TPU v7x, 32 devices: a whole 2x2x4 slice. The times are simulated.
32 devices in a mesh: grp: 8 (over y, x, core), dom: 4 (over z).
Axes of the slice: x: 2, y: 2, z: 4, core: 2. Of those that a mesh axis runs over, the one named last changes fastest.
Arguments:
- surplus: float32 [128, 512, 512], P('grp', 'dom'), may hold values from -0.4 to 0.4
- block_ids: int32 [128, 512], P('grp', 'dom'), may hold values from 0 to 4095, as said below
- coef: int32 [128], P('grp'), may hold values from -4 to 6, as said below
Outputs:
- updated: float32 [128, 512, 512], P('grp', 'dom')
Inputs may be any that keep to these rules, and one draw needn't show every extreme that they name: `block_ids`: for each grid, the slots in columns d * 128 to (d + 1) * 128 - 1 hold 128 different numbers from d * 1024 to (d + 1) * 1024 - 1. `coef`: each coefficient is one of 1, -4, 6.
All inputs are finite; a program needn't handle non-finite values.
Results may differ from a plain program's by a relative error of at most 0.000071.
Values sent between devices are 32-bit elements; how exact they have to be, the bound alone decides.
A program may use at most 64 MiB of HBM per device.

v0:
```python
import jax
import jax.numpy as jnp
from jax import lax
from jax.sharding import PartitionSpec as P

NBD = 1024


def local(surplus, block_ids, coef):
    offset = lax.axis_index("dom") * NBD
    local_ids = block_ids - offset
    columns = lax.broadcasted_iota(jnp.int32, (1, 1, NBD), 2)
    onehot = (local_ids[:, :, None] == columns).astype(jnp.float32)
    scaled = surplus * coef.astype(jnp.float32)[:, None, None]
    partial_sum = jnp.einsum("gkn,gkb->nb", onehot, scaled, precision=lax.Precision.HIGHEST)
    combined = lax.psum(partial_sum, "grp")
    return jnp.einsum("gkn,nb->gkb", onehot, combined, precision=lax.Precision.HIGHEST)


def solution(mesh):
    return jax.shard_map(
        local,
        mesh=mesh,
        in_specs=(P("grp", "dom", None), P("grp", "dom"), P("grp")),
        out_specs=P("grp", "dom", None),
        check_vma=False,
    )
```

profile of v0, /device:TPU:0, one launch (start us, length us, event | category | flops | bytes accessed | tf_op | source)
XLA Modules:
  0.0 106.6 jit_solution(6642148042508687133)
XLA Ops:
  6.5 0.0 all-reduce.2.cloned.1.call-start
  6.5 0.7 convert_element_type.4
  7.2 0.7 broadcast_subtract_fusion
  7.9 16.8 %fusion.7 = f32[1024,512]{1,0:T(8,128)} fusion(f32[16,128,512]{2,1,0:T(8,128)} %param.3, f32[16]{0:T(128)S(1)} %convert_element_type.4, s32[16,128]{1,0:T(8,128)S(1)} %broadcast_subtract_fusion), kind=kOutput, calls=%fused_computation.8 | convolution fusion | flops 12888047616 | bytes 6299712 | tf_op jit(solution)/shard_map/gkn,gkb->nb/dot_general | solution.py:15
  24.7 0.0 all-reduce.2.cloned.1.call-update
  24.7 64.6 %all-reduce.2.cloned.1.call-done = f32[1024,512]{1,0:T(8,128)} async-done(((f32[1024,512]{1,0:T(8,128)}), f32[1024,512]{1,0:T(8,128)}) %all-reduce.2.cloned.1.call-update) | async-done | bytes 2097168 | tf_op jit(solution)/shard_map/psum | solution.py:16
  89.3 10.4 %fusion = f32[16,128,512]{2,1,0:T(8,128)} fusion(s32[16,128]{1,0:T(8,128)S(1)} %broadcast_subtract_fusion, f32[1024,512]{1,0:T(8,128)} %all-reduce.2.cloned.1.call-done), kind=kOutput, calls=%fused_computation.1 | convolution fusion | flops 12886999040 | bytes 6299648 | tf_op jit(solution)/shard_map/gkn,nb->gkb/dot_general | solution.py:17
Async XLA Ops:
  6.5 82.8 %all-reduce.2.cloned.1.call-start = ((), (), s32[]{:S(2)}) async-start(), calls=%async_computation | async-start | bytes 4194304 | tf_op jit(solution)/shard_map/psum | solution.py:16
Sparse Core Ops, SparseCore 0:
  24.8 64.4 all-reduce.1
where the time goes:
time: 107 us
  waiting for transfers between devices  64.7 us (60%)
  matrix products  27.2 us (25%)
  between operations  13.4 us (13%)
  other arithmetic  1.36 us (1%)
    psum x1, waiting for transfers between devices, local(): combined = lax.psum(partial_sum, 'grp')  64.6 us
    dot_general x1, matrix products, local(): jnp.einsum('gkn,gkb->nb', onehot, scaled, precision=lax.Precision.HIGHEST)  16.8 us
    dot_general x1, matrix products, local(): jnp.einsum('gkn,nb->gkb', onehot, combined, precision=lax.Precision.HIGHEST)  10.4 us
  transfers between devices with their start and end apart: 1, of which 1 were waited for; matrix products, arithmetic and copies ran while one was open for 0% of the time, Pallas kernels for 0%

commit v1 on v0

--- a/solution.py
+++ b/solution.py
@@ -13,7 +13,7 @@
     onehot = (local_ids[:, :, None] == columns).astype(jnp.float32)
     scaled = surplus * coef.astype(jnp.float32)[:, None, None]
     partial_sum = jnp.einsum("gkn,gkb->nb", onehot, scaled, precision=lax.Precision.HIGHEST)
-    combined = lax.psum(partial_sum, "grp")
+    combined = jnp.sum(lax.all_gather(partial_sum, axis_name="grp"), 0)
     return jnp.einsum("gkn,nb->gkb", onehot, combined, precision=lax.Precision.HIGHEST)
 
 

time: 107 us -> 141 us (1.32)
  waiting for transfers between devices: 64.7 us -> 92.6 us
  other arithmetic: 1.36 us -> 9.53 us
  matrix products: 27.2 us -> 25.3 us
    all_gather x0 -> x1, waiting for transfers between devices: none -> 92.6 us  [local(): combined = jnp.sum(lax.all_gather(partial_sum, axis_name='grp'), 0)]
    psum x1 -> x0, waiting for transfers between devices: 64.6 us -> none  [local(): combined = lax.psum(partial_sum, 'grp')]
    reduce_sum x0 -> x1, other arithmetic: none -> 8.17 us  [local(): combined = jnp.sum(lax.all_gather(partial_sum, axis_name='grp'), 0)]
    dot_general x1, matrix products: 10.4 us -> 8.55 us  [local(): jnp.einsum('gkn,nb->gkb', onehot, combined, precision=lax.Precision.HIGHEST)]
where the time goes in v1:
time: 141 us
  waiting for transfers between devices  92.6 us (66%)
  matrix products  25.3 us (18%)
  between operations  13.4 us (10%)
  other arithmetic  9.53 us (7%)
    all_gather x1, waiting for transfers between devices, local(): combined = jnp.sum(lax.all_gather(partial_sum, axis_name='grp'), 0)  92.6 us
    dot_general x1, matrix products, local(): jnp.einsum('gkn,gkb->nb', onehot, scaled, precision=lax.Precision.HIGHEST)  16.8 us
    dot_general x1, matrix products, local(): jnp.einsum('gkn,nb->gkb', onehot, combined, precision=lax.Precision.HIGHEST)  8.55 us
    reduce_sum x1, other arithmetic, local(): combined = jnp.sum(lax.all_gather(partial_sum, axis_name='grp'), 0)  8.17 us
  transfers between devices with their start and end apart: 1, of which 1 were waited for; matrix products, arithmetic and copies ran while one was open for 0% of the time, Pallas kernels for 0%

profile of v1, /device:TPU:0, one launch (start us, length us, event | category | flops | bytes accessed | tf_op | source)
XLA Modules:
  0.0 140.9 jit_solution(7884906933654413628)
XLA Ops:
  6.5 0.0 all-gather.3.cloned.1.call-start
  6.5 0.7 convert_element_type.4
  7.2 0.7 broadcast_subtract_fusion
  7.9 16.8 %fusion.7 = f32[1024,512]{1,0:T(8,128)} fusion(f32[16,128,512]{2,1,0:T(8,128)} %param.3, f32[16]{0:T(128)S(1)} %convert_element_type.4, s32[16,128]{1,0:T(8,128)S(1)} %broadcast_subtract_fusion), kind=kOutput, calls=%fused_computation.8 | convolution fusion | flops 12888047616 | bytes 6299712 | tf_op jit(solution)/shard_map/gkn,gkb->nb/dot_general | solution.py:15
  24.7 0.0 all-gather.3.cloned.1.call-update
  24.7 92.6 %all-gather.3.cloned.1.call-done = f32[8192,512]{1,0:T(8,128)} async-done(((f32[1024,512]{1,0:T(8,128)}), f32[8192,512]{1,0:T(8,128)}) %all-gather.3.cloned.1.call-update) | async-done | bytes 16777232 | tf_op jit(solution)/shard_map/all_gather | solution.py:16
  117.3 8.2 %reduce_sum.9 = f32[1024,512]{1,0:T(8,128)S(1)} reduce(f32[8,1024,512]{2,1,0:T(8,128)} %bitcast.6, f32[]{:T(128)} %constant.2.clone.1), dimensions={0}, to_apply=%region_0.0 | reduce | flops 3670016 | bytes 18874372 | tf_op jit(solution)/shard_map/reduce_sum | solution.py:16
  125.5 8.6 %fusion = f32[16,128,512]{2,1,0:T(8,128)} fusion(s32[16,128]{1,0:T(8,128)S(1)} %broadcast_subtract_fusion, f32[1024,512]{1,0:T(8,128)S(1)} %reduce_sum.9), kind=kOutput, calls=%fused_computation.1 | convolution fusion | flops 12886999040 | bytes 6299648 | tf_op jit(solution)/shard_map/gkn,nb->gkb/dot_general | solution.py:17
Async XLA Ops:
  6.5 110.8 %all-gather.3.cloned.1.call-start = ((), (), s32[]{:S(2)}) async-start(), calls=%async_computation | async-start | bytes 18874368 | tf_op jit(solution)/shard_map/all_gather | solution.py:16
Sparse Core Ops, SparseCore 0:
  24.8 92.4 all-gather.2
